TPU v7x, 32 devices: a whole 2x2x4 slice. The times are simulated.
32 devices in a mesh: pipe: 2 (over x), expert: 8 (over z, core), dp: 2 (over y).
Axes of the slice: x: 2, y: 2, z: 4, core: 2. Of those that a mesh axis runs over, the one named last changes fastest.
Arguments:
- tokens: bfloat16 [2, 2048, 2048], P('pipe', ('expert', 'dp')), may hold values from -6 to 6
- cotangent: bfloat16 [2, 2048, 2048], P('pipe', ('expert', 'dp')), may hold values from -6 to 6
- norm_gain: float32 [2, 2048], P('pipe'), may hold values from 0.5 to 1.5
- first_ids: int32 [2, 2048, 2], P('pipe', ('expert', 'dp')), may hold values from 0 to 3, all different within a row; in each aligned block of 128 rows (0 to 127, 128 to 255, ..., all dimensions but the last counted through in order) at most 72 rows name the same one
- first_gates: float32 [2, 2048, 2], P('pipe', ('expert', 'dp')), may hold values from 0.1 to 1
- second_ids: int32 [2, 2048, 2], P('pipe', ('expert', 'dp')), may hold values from 0 to 3, all different within a row; in each aligned block of 128 rows (0 to 127, 128 to 255, ..., all dimensions but the last counted through in order) at most 72 rows name the same one
- second_gates: float32 [2, 2048, 2], P('pipe', ('expert', 'dp')), may hold values from 0.1 to 1
- new_slot: int32 [2, 4], P('pipe'), may hold values from 0 to 3, each once within a row
- inner_weight: float32 [2, 8, 2, 2048, 384], P('pipe', 'expert', None, 'dp'), may hold values from -0.125 to 0.125
- outer_weight: float32 [2, 8, 384, 2048], P('pipe', 'expert', None, 'dp'), may hold values from -0.21875 to 0.21875
- inner_mean: bfloat16 [2, 8, 2, 2048, 384], P('pipe', 'expert', None, 'dp'), may hold values from -60 to 60
- outer_mean: bfloat16 [2, 8, 384, 2048], P('pipe', 'expert', None, 'dp'), may hold values from -60 to 60
- inner_square: bfloat16 [2, 8, 2, 2048, 384], P('pipe', 'expert', None, 'dp'), may hold values from 10 to 1000
- outer_square: bfloat16 [2, 8, 384, 2048], P('pipe', 'expert', None, 'dp'), may hold values from 10 to 1000
Outputs:
- layer_out: bfloat16 [2, 2048, 2048], P('pipe', ('expert', 'dp'))
- weight_inner: float32 [2, 8, 2, 2048, 384], P('pipe', 'expert', None, 'dp')
- weight_outer: float32 [2, 8, 384, 2048], P('pipe', 'expert', None, 'dp')
- mean_inner: bfloat16 [2, 8, 2, 2048, 384], P('pipe', 'expert', None, 'dp')
- mean_outer: bfloat16 [2, 8, 384, 2048], P('pipe', 'expert', None, 'dp')
- square_inner: bfloat16 [2, 8, 2, 2048, 384], P('pipe', 'expert', None, 'dp')
- square_outer: bfloat16 [2, 8, 384, 2048], P('pipe', 'expert', None, 'dp')
Inputs may be any that keep to these rules, and one draw needn't show every extreme that they name: `first_ids`: each token names 2 different experts. Within the rows of one device no expert is named more than 72 times, and some device names some expert exactly 72 times. `second_ids`: as first_ids. `new_slot`: for each section, a permutation of the 4 experts.
All inputs are finite; a program needn't handle non-finite values.
Results may differ from a plain program's by a relative error of at most 0.008.
Values may be sent and summed in bfloat16 or wider, within the bound.
A program may use at most 128 MiB of HBM per device.

v0:
```python
import jax
import jax.numpy as jnp
from jax import lax
from jax.sharding import PartitionSpec as P

norm_eps = 1e-06
learn_rate = 0.001
beta_one = 0.9
beta_two = 0.95
adam_eps = 1e-08
bias_one = 0.999973438601112
bias_two = 0.994079470779667


def for_sending(array):

    def short(part):
        return part.astype(jnp.bfloat16) if part.dtype == jnp.float32 else part

    return jax.tree.map(short, array)


def passed_along(block, axis, distance):
    devices = range(lax.axis_size(axis))
    route = [((i - distance) % len(devices), i) for i in devices]
    return lax.ppermute(block, axis, route)


def normed(values, gain_row):
    widened = values.astype(jnp.float32)
    inverse_rms = lax.rsqrt(jnp.mean(widened * widened, axis=-1, keepdims=True) + norm_eps)
    return (widened * inverse_rms * gain_row).astype(jnp.bfloat16)


def silu_parts(gate_proj):
    logistic = jax.nn.sigmoid(gate_proj)
    return (gate_proj * logistic, logistic * (1.0 + gate_proj * (1.0 - logistic)))


def half_forward(token_rows, inner_full, outer_full):
    gate_proj = jnp.dot(token_rows, inner_full[0], preferred_element_type=jnp.float32)
    up_proj = jnp.dot(token_rows, inner_full[1], preferred_element_type=jnp.float32)
    activity = (silu_parts(gate_proj)[0] * up_proj).astype(jnp.bfloat16)
    half_out = jnp.dot(activity, outer_full, preferred_element_type=jnp.float32).astype(
        jnp.bfloat16
    )
    return (half_out, activity, gate_proj, up_proj)


def half_backward(token_rows, grad_rows, outer_full, activity, gate_proj, up_proj):
    grad_outer = jnp.dot(activity.T, grad_rows, preferred_element_type=jnp.float32)
    d_active = jnp.dot(grad_rows, outer_full.T, preferred_element_type=jnp.float32)
    swish_value, swish_slope = silu_parts(gate_proj)
    d_gate = (d_active * up_proj * swish_slope).astype(jnp.bfloat16)
    d_upper = (d_active * swish_value).astype(jnp.bfloat16)
    grad_gate = jnp.dot(token_rows.T, d_gate, preferred_element_type=jnp.float32)
    grad_upper = jnp.dot(token_rows.T, d_upper, preferred_element_type=jnp.float32)
    return (jnp.stack([grad_gate, grad_upper]), grad_outer)


def slot_index(ids, pair_of, capacity):
    flattened = ids.reshape(-1)
    expert_row = jnp.arange(pair_of.shape[0], dtype=jnp.int32)
    onehot = (flattened[:, None] == expert_row[None, :]).astype(jnp.int32)
    ranking = jnp.sum((jnp.cumsum(onehot, axis=0) - 1) * onehot, axis=1)
    target = jnp.sum(onehot * pair_of[None, :], axis=1)
    return (target * capacity + ranking).reshape(ids.shape)


def selection(slots, values, total_slots):
    positions = jnp.arange(total_slots, dtype=jnp.int32)
    result = jnp.zeros((total_slots, slots.shape[0]), jnp.float32)
    for column in range(slots.shape[1]):
        result = result + jnp.where(
            slots[:, column][None, :] == positions[:, None], values[:, column][None, :], 0.0
        )
    return result


def both_halves(packed, pair_count, capacity):
    return jnp.repeat(packed.reshape(pair_count, capacity, packed.shape[-1]), 2, axis=0)


def gather_weights(inner_master, outer_master):
    inner_full, outer_full = (
        lax.all_gather(inner_master.astype(jnp.bfloat16), "dp", axis=3, tiled=True),
        lax.all_gather(outer_master.astype(jnp.bfloat16), "dp", axis=3, tiled=True),
    )
    return (inner_full[0, 0], outer_full[0, 0])


def forward_layer(token_rows, gain_row, ids, gates, pair_of, inner_full, outer_full, capacity):
    pair_count = pair_of.shape[0]
    normal = normed(token_rows, gain_row)
    slots = slot_index(ids, pair_of, capacity)
    picker = selection(slots, jnp.ones(slots.shape, jnp.float32), pair_count * capacity).astype(
        jnp.bfloat16
    )
    packed = jnp.dot(picker, normal, preferred_element_type=jnp.float32).astype(jnp.bfloat16)
    send_rows = both_halves(packed, pair_count, capacity)
    arrived = lax.all_to_all(send_rows, "expert", split_axis=0, concat_axis=0, tiled=True)
    shape = arrived.shape
    half_out, activity, gate_proj, up_proj = half_forward(
        arrived.reshape(-1, shape[-1]), inner_full, outer_full
    )
    hidden = activity.shape[-1]
    half_out, arrived, activity, gate_proj, up_proj = (
        half_out.reshape(shape),
        arrived,
        activity.reshape(shape[0], shape[1], hidden),
        gate_proj.reshape(shape[0], shape[1], hidden),
        up_proj.reshape(shape[0], shape[1], hidden),
    )
    returned = lax.all_to_all(half_out, "expert", split_axis=0, concat_axis=0, tiled=True)
    summed = returned.astype(jnp.float32).reshape(pair_count, 2, capacity, -1).sum(axis=1)
    summed = summed.reshape(pair_count * capacity, -1)
    picked = summed[slots]
    mixed_rows = token_rows.astype(jnp.float32) + jnp.sum(gates[..., None] * picked, axis=1)
    return (mixed_rows.astype(jnp.bfloat16), (slots, arrived, activity, gate_proj, up_proj))


def adam_step(weight, mean, square, grads):
    mean_new = (beta_one * mean.astype(jnp.float32) + (1.0 - beta_one) * grads).astype(jnp.bfloat16)
    square_new = (beta_two * square.astype(jnp.float32) + (1.0 - beta_two) * grads * grads).astype(
        jnp.bfloat16
    )
    mean_wide = lax.optimization_barrier(mean_new).astype(jnp.float32)
    square_wide = lax.optimization_barrier(square_new).astype(jnp.float32)
    update = mean_wide / bias_one / (jnp.sqrt(square_wide / bias_two) + adam_eps)
    return (weight - learn_rate * update, mean_new, square_new)


def relocate_master(inner_master, outer_master, source):
    devices = source.shape[0]
    inner_spread, outer_spread = (
        lax.all_to_all(
            inner_master.reshape(devices, -1).astype(jnp.bfloat16),
            "expert",
            split_axis=0,
            concat_axis=0,
            tiled=True,
        ).astype(jnp.float32),
        lax.all_to_all(
            outer_master.reshape(devices, -1).astype(jnp.bfloat16),
            "expert",
            split_axis=0,
            concat_axis=0,
            tiled=True,
        ).astype(jnp.float32),
    )
    inner_order = jnp.take(inner_spread, source, axis=0)
    outer_order = jnp.take(outer_spread, source, axis=0)
    inner_back, outer_back = (
        lax.all_to_all(
            for_sending(inner_order), "expert", split_axis=0, concat_axis=0, tiled=True
        ).astype(inner_order.dtype),
        lax.all_to_all(
            for_sending(outer_order), "expert", split_axis=0, concat_axis=0, tiled=True
        ).astype(outer_order.dtype),
    )
    return (inner_back.reshape(inner_master.shape), outer_back.reshape(outer_master.shape))


def relocate_moments(first_inner, first_outer, second_inner, second_outer, source):
    devices = source.shape[0]
    spread = (
        lax.all_to_all(
            first_inner.reshape(devices, -1), "expert", split_axis=0, concat_axis=0, tiled=True
        ),
        lax.all_to_all(
            first_outer.reshape(devices, -1), "expert", split_axis=0, concat_axis=0, tiled=True
        ),
        lax.all_to_all(
            second_inner.reshape(devices, -1), "expert", split_axis=0, concat_axis=0, tiled=True
        ),
        lax.all_to_all(
            second_outer.reshape(devices, -1), "expert", split_axis=0, concat_axis=0, tiled=True
        ),
    )
    ordered = [jnp.take(member, source, axis=0) for member in spread]
    back = (
        lax.all_to_all(ordered[0], "expert", split_axis=0, concat_axis=0, tiled=True),
        lax.all_to_all(ordered[1], "expert", split_axis=0, concat_axis=0, tiled=True),
        lax.all_to_all(ordered[2], "expert", split_axis=0, concat_axis=0, tiled=True),
        lax.all_to_all(ordered[3], "expert", split_axis=0, concat_axis=0, tiled=True),
    )
    return (
        back[0].reshape(first_inner.shape),
        back[1].reshape(first_outer.shape),
        back[2].reshape(second_inner.shape),
        back[3].reshape(second_outer.shape),
    )


def per_device(
    tokens,
    cotangent,
    norm_gain,
    first_ids,
    first_gates,
    second_ids,
    second_gates,
    new_slot,
    inner_weight,
    outer_weight,
    inner_mean,
    outer_mean,
    inner_square,
    outer_square,
):
    pair_count = new_slot.shape[1]
    rows_here = tokens.shape[1]
    top_count = first_ids.shape[2]
    width = tokens.shape[2]
    usual = rows_here * top_count // pair_count
    capacity = min(rows_here, usual + usual // 8)
    gain_row = norm_gain[0]
    identity_map = jnp.arange(pair_count, dtype=jnp.int32)
    inner_full, outer_full = gather_weights(inner_weight, outer_weight)
    first_out, saved = forward_layer(
        tokens[0],
        gain_row,
        first_ids[0],
        first_gates[0],
        identity_map,
        inner_full,
        outer_full,
        capacity,
    )
    slots, arrived, activity, gate_proj, up_proj = saved
    weighting = selection(slots, first_gates[0], pair_count * capacity)
    grad_packed = jnp.dot(
        weighting, cotangent[0].astype(jnp.float32), precision=lax.Precision.HIGHEST
    ).astype(jnp.bfloat16)
    grad_send = both_halves(grad_packed, pair_count, capacity)
    grad_arrived = lax.all_to_all(grad_send, "expert", split_axis=0, concat_axis=0, tiled=True)
    hidden = activity.shape[-1]
    grad_inner, grad_outer = half_backward(
        arrived.reshape(-1, width),
        grad_arrived.reshape(-1, width),
        outer_full,
        activity.reshape(-1, hidden),
        gate_proj.reshape(-1, hidden),
        up_proj.reshape(-1, hidden),
    )
    sum_inner, sum_outer = (
        lax.psum_scatter(
            grad_inner[None, None].astype(jnp.bfloat16), "dp", scatter_dimension=3, tiled=True
        ).astype(jnp.float32),
        lax.psum_scatter(
            grad_outer[None, None].astype(jnp.bfloat16), "dp", scatter_dimension=3, tiled=True
        ).astype(jnp.float32),
    )
    stepped_inner, mean_in_new, square_in_new = adam_step(
        inner_weight, inner_mean, inner_square, sum_inner
    )
    stepped_outer, mean_out_new, square_out_new = adam_step(
        outer_weight, outer_mean, outer_square, sum_outer
    )
    new_pairs = new_slot[0]
    inverse = jnp.sum(
        jnp.where(new_pairs[:, None] == identity_map[None, :], identity_map[:, None], 0), axis=0
    )
    device_ids = jnp.arange(2 * pair_count, dtype=jnp.int32)
    source = 2 * jnp.repeat(inverse, 2) + device_ids % 2
    moved_inner, moved_outer = relocate_master(stepped_inner, stepped_outer, source)
    moved_mean_in, moved_mean_out, moved_square_in, moved_square_out = relocate_moments(
        mean_in_new, mean_out_new, square_in_new, square_out_new, source
    )
    inner_two, outer_two = gather_weights(moved_inner, moved_outer)
    shifted = passed_along(first_out, "pipe", 1)
    second_out, unused = forward_layer(
        shifted, gain_row, second_ids[0], second_gates[0], new_pairs, inner_two, outer_two, capacity
    )
    return (
        second_out[None],
        moved_inner,
        moved_outer,
        moved_mean_in,
        moved_mean_out,
        moved_square_in,
        moved_square_out,
    )


def solution(mesh):
    return jax.shard_map(
        per_device,
        mesh=mesh,
        in_specs=(
            P("pipe", ("expert", "dp"), None),
            P("pipe", ("expert", "dp"), None),
            P("pipe", None),
            P("pipe", ("expert", "dp"), None),
            P("pipe", ("expert", "dp"), None),
            P("pipe", ("expert", "dp"), None),
            P("pipe", ("expert", "dp"), None),
            P("pipe", None),
            P("pipe", "expert", None, "dp", None),
            P("pipe", "expert", None, "dp"),
            P("pipe", "expert", None, "dp", None),
            P("pipe", "expert", None, "dp"),
            P("pipe", "expert", None, "dp", None),
            P("pipe", "expert", None, "dp"),
        ),
        out_specs=(
            P("pipe", ("expert", "dp"), None),
            P("pipe", "expert", None, "dp", None),
            P("pipe", "expert", None, "dp"),
            P("pipe", "expert", None, "dp", None),
            P("pipe", "expert", None, "dp"),
            P("pipe", "expert", None, "dp", None),
            P("pipe", "expert", None, "dp"),
        ),
        check_vma=False,
    )
```

profile of v0, /device:TPU:1, one launch (start us, length us, event | category | flops | bytes accessed | tf_op | source)
XLA Modules:
  0.0 822.0 jit_solution(1338081276106680702)
XLA Ops:
  14.8 6.5 all-to-all-start
  22.4 52.7 %all-to-all-done = bf16[8,72,2048]{2,1,0:T(8,128)(2,1)} async-done(((bf16[8,72,2048]{2,1,0:T(8,128)(2,1)}), bf16[8,72,2048]{2,1,0:T(8,128)(2,1)}, u32[]{:S(2)}, u32[]{:S(2)}) %all-to-all-start) | async-done | bytes 2359328 | tf_op jit(solution)/shard_map/all_to_all | solution.py:101
  84.0 46.8 %all-gather.5.cloned.1.call-done = bf16[1,1,2,2048,384]{4,3,2,1,0:T(8,128)(2,1)} async-done(((bf16[1,1,2,1024,384]{4,3,2,1,0:T(8,128)(2,1)}), bf16[1,1,2,2048,384]{4,3,2,1,0:T(8,128)(2,1)}) %all-gather.5.cloned.1.call-update) | async-done | bytes 3145744 | tf_op jit(solution)/shard_map/all_gather | solution.py:86
  143.3 26.3 %reduce-scatter.5.cloned.1.call-done = bf16[1,1,384,1024]{3,2,1,0:T(8,128)(2,1)} async-done(((bf16[1,1,384,2048]{3,2,1,0:T(8,128)(2,1)}), bf16[1,1,384,1024]{3,2,1,0:T(8,128)(2,1)}) %reduce-scatter.5.cloned.1.call-update) | async-done | bytes 786448 | tf_op jit(solution)/shard_map/reduce_scatter | solution.py:250
  176.7 6.3 reduce.14
  185.6 5.8 all-to-all-start.6
  199.1 12.4 %all-to-all-done.6 = bf16[8,2,24576]{2,1,0:T(2,128)(2,1)} async-done(((bf16[8,2,24576]{2,1,0:T(2,128)(2,1)}), bf16[8,2,24576]{2,1,0:T(2,128)(2,1)}, u32[]{:S(2)}, u32[]{:S(2)}) %all-to-all-start.6) | async-done | bytes 786464 | tf_op jit(solution)/shard_map/all_to_all | solution.py:143
  245.6 15.5 %all-to-all-done.11 = bf16[8,2,24576]{2,1,0:T(2,128)(2,1)} async-done(((bf16[8,2,24576]{2,1,0:T(2,128)(2,1)}), bf16[8,2,24576]{2,1,0:T(2,128)(2,1)}, u32[]{:S(2)}, u32[]{:S(2)}) %all-to-all-start.11) | async-done | bytes 786464 | tf_op jit(solution)/shard_map/all_to_all | solution.py:170
  297.0 17.2 %all-to-all-done.12 = bf16[8,2,24576]{2,1,0:T(2,128)(2,1)S(1)} async-done(((bf16[8,2,24576]{2,1,0:T(2,128)(2,1)}), bf16[8,2,24576]{2,1,0:T(2,128)(2,1)S(1)}, u32[]{:S(2)}, u32[]{:S(2)}) %all-to-all-start.12) | async-done | bytes 786464 | tf_op jit(solution)/shard_map/all_to_all | solution.py:183
  322.9 15.8 %all-to-all-done.16 = bf16[8,2,24576]{2,1,0:T(2,128)(2,1)S(1)} async-done(((bf16[8,2,24576]{2,1,0:T(2,128)(2,1)}), bf16[8,2,24576]{2,1,0:T(2,128)(2,1)S(1)}, u32[]{:S(2)}, u32[]{:S(2)}) %all-to-all-start.16) | async-done | bytes 786464 | tf_op jit(solution)/shard_map/all_to_all | solution.py:185
  351.3 6.3 convert_element_type.273
  357.6 12.9 %reduce.16 = bf16[8,98304]{1,0:T(8,128)(2,1)} reduce(bf16[8,1,98304]{2,1,0:T(2,128)(2,1)} %convert_element_type.273, bf16[]{:T(256)} %broadcast.417), dimensions={1}, to_apply=%convert_element_type.273.reduce_sub_computation | reduce | bytes 3145730 | tf_op jit(solution)/shard_map/convert_element_type | solution.py:137
  374.4 24.2 %all-to-all-done.1 = bf16[8,72,2048]{2,1,0:T(8,128)(2,1)} async-done(((bf16[8,72,2048]{2,1,0:T(8,128)(2,1)}), bf16[8,72,2048]{2,1,0:T(8,128)(2,1)}, u32[]{:S(2)}, u32[]{:S(2)}) %all-to-all-start.1) | async-done | bytes 2359328 | tf_op jit(solution)/shard_map/all_to_all | solution.py:114
  407.4 11.8 %reduce.18 = bf16[8,98304]{1,0:T(8,128)(2,1)S(1)} reduce(bf16[8,1,98304]{2,1,0:T(2,128)(2,1)} %all_to_all.124, bf16[]{:T(256)} %broadcast.417), dimensions={1}, to_apply=%all_to_all.124.reduce_sub_computation | reduce | bytes 3145730 | tf_op jit(solution)/shard_map/all_to_all | solution.py:173
  421.6 19.2 %all-to-all-done.4 = bf16[8,2,49152]{2,1,0:T(2,128)(2,1)} async-done(((bf16[8,2,49152]{2,1,0:T(2,128)(2,1)}), bf16[8,2,49152]{2,1,0:T(2,128)(2,1)}, u32[]{:S(2)}, u32[]{:S(2)}) %all-to-all-start.4) | async-done | bytes 1572896 | tf_op jit(solution)/shard_map/all_to_all | solution.py:136
  449.1 11.8 %reduce.19 = bf16[8,98304]{1,0:T(8,128)(2,1)S(1)} reduce(bf16[8,1,98304]{2,1,0:T(2,128)(2,1)} %all_to_all.122, bf16[]{:T(256)} %broadcast.417), dimensions={1}, to_apply=%all_to_all.122.reduce_sub_computation | reduce | bytes 3145730 | tf_op jit(solution)/shard_map/all_to_all | solution.py:167
  463.4 19.0 %all-to-all-done.13 = bf16[8,2,49152]{2,1,0:T(2,128)(2,1)S(1)} async-done(((bf16[8,2,49152]{2,1,0:T(2,128)(2,1)}), bf16[8,2,49152]{2,1,0:T(2,128)(2,1)S(1)}, u32[]{:S(2)}, u32[]{:S(2)}) %all-to-all-start.13) | async-done | bytes 1572896 | tf_op jit(solution)/shard_map/all_to_all | solution.py:173
  504.1 11.6 %collective-permute-done = bf16[128,2048]{1,0:T(8,128)(2,1)S(1)} collective-permute-done((bf16[128,2048]{1,0:T(8,128)(2,1)S(1)}, bf16[128,2048]{1,0:T(8,128)(2,1)S(1)}, u32[]{:S(2)}, u32[]{:S(2)}) %collective-permute-start) | collective-permute-done | bytes 524320 | tf_op jit(solution)/shard_map/ppermute | solution.py:26
  517.5 6.3 reshape.597
  532.0 5.9 all-to-all-start.2
  551.7 6.3 reshape.601
  564.3 27.3 %all-to-all-done.2 = bf16[8,72,2048]{2,1,0:T(8,128)(2,1)} async-done(((bf16[8,72,2048]{2,1,0:T(8,128)(2,1)}), bf16[8,72,2048]{2,1,0:T(8,128)(2,1)}, u32[]{:S(2)}, u32[]{:S(2)}) %all-to-all-start.2) | async-done | bytes 2359328 | tf_op jit(solution)/shard_map/all_to_all | solution.py:101
  605.2 27.7 %all-to-all-done.5 = bf16[8,2,49152]{2,1,0:T(2,128)(2,1)S(1)} async-done(((bf16[8,2,49152]{2,1,0:T(2,128)(2,1)}), bf16[8,2,49152]{2,1,0:T(2,128)(2,1)S(1)}, u32[]{:S(2)}, u32[]{:S(2)}) %all-to-all-start.5) | async-done | bytes 1572896 | tf_op jit(solution)/shard_map/all_to_all | solution.py:154
  644.1 10.7 %reduce.4 = bf16[8,98304]{1,0:T(8,128)(2,1)} reduce(bf16[8,1,98304]{2,1,0:T(2,128)(2,1)S(1)} %reshape.599, bf16[]{:T(256)} %constant.142), dimensions={1}, to_apply=%all_to_all.96.reduce_sub_computation | reduce | bytes 3145730 | tf_op jit(solution)/shard_map/all_to_all | solution.py:154
  664.3 11.9 %all-to-all-done.10 = bf16[8,2,49152]{2,1,0:T(2,128)(2,1)} async-done(((bf16[8,2,49152]{2,1,0:T(2,128)(2,1)}), bf16[8,2,49152]{2,1,0:T(2,128)(2,1)}, u32[]{:S(2)}, u32[]{:S(2)}) %all-to-all-start.10) | async-done | bytes 1572896 | tf_op jit(solution)/shard_map/all_to_all | solution.py:182
  684.7 5.7 reduce.5
  692.8 10.1 %all-gather.9.cloned.1.call-done = bf16[1,1,2,2048,384]{4,3,2,1,0:T(8,128)(2,1)} async-done(((bf16[1,1,2,1024,384]{4,3,2,1,0:T(8,128)(2,1)}), bf16[1,1,2,2048,384]{4,3,2,1,0:T(8,128)(2,1)}) %all-gather.9.cloned.1.call-update) | async-done | bytes 3145744 | tf_op jit(solution)/shard_map/all_gather | solution.py:86
  706.4 25.7 %all-gather.11.cloned.1.call-done = bf16[1,1,384,2048]{3,2,1,0:T(8,128)(2,1)} async-done(((bf16[1,1,384,1024]{3,2,1,0:T(8,128)(2,1)}), bf16[1,1,384,2048]{3,2,1,0:T(8,128)(2,1)}) %all-gather.11.cloned.1.call-update) | async-done | bytes 1572880 | tf_op jit(solution)/shard_map/all_gather | solution.py:87
  732.1 6.7 convolution_convert_fusion
  739.9 5.7 all-to-all-start.8
  769.9 10.7 %reduce.6 = bf16[8,98304]{1,0:T(8,128)(2,1)} reduce(bf16[8,1,98304]{2,1,0:T(2,128)(2,1)S(1)} %reshape.603, bf16[]{:T(256)} %constant.142), dimensions={1}, to_apply=%all_to_all.106.reduce_sub_computation | reduce | bytes 3145730 | tf_op jit(solution)/shard_map/all_to_all | solution.py:182
  789.0 10.8 %reduce.8 = bf16[8,98304]{1,0:T(8,128)(2,1)} reduce(bf16[8,1,98304]{2,1,0:T(2,128)(2,1)S(1)} %reshape.611, bf16[]{:T(256)} %constant.142), dimensions={1}, to_apply=%all_to_all.116.reduce_sub_computation | reduce | bytes 3145730 | tf_op jit(solution)/shard_map/all_to_all | solution.py:184
  (240 shorter events, 313.5 us)
Async XLA Ops:
  7.2 14.2 %copy-start = (bf16[1,128,2048]{2,1,0:T(8,128)(2,1)S(1)}, bf16[1,128,2048]{2,1,0:T(8,128)(2,1)}, u32[]{:S(2)}) copy-start(bf16[1,128,2048]{2,1,0:T(8,128)(2,1)} %param.19) | copy-start | bytes 1572868
  14.8 60.3 %all-to-all-start = ((bf16[8,72,2048]{2,1,0:T(8,128)(2,1)}), bf16[8,72,2048]{2,1,0:T(8,128)(2,1)}, u32[]{:S(2)}, u32[]{:S(2)}) async-start(bf16[8,72,2048]{2,1,0:T(8,128)(2,1)} %bitcast.7), calls=%async_computation | async-start | bytes 4718592 | tf_op jit(solution)/shard_map/all_to_all | solution.py:101
  76.8 62.0 %all-to-all-start.3 = ((bf16[8,72,2048]{2,1,0:T(8,128)(2,1)}), bf16[8,72,2048]{2,1,0:T(8,128)(2,1)}, u32[]{:S(2)}, u32[]{:S(2)}) async-start(bf16[8,72,2048]{2,1,0:T(8,128)(2,1)} %bitcast.176), calls=%async_computation.3 | async-start | bytes 4718592 | tf_op jit(solution)/shard_map/all_to_all | solution.py:236
  82.3 48.5 %all-gather.5.cloned.1.call-start = ((), (), s32[]{:S(2)}) async-start(), calls=%async_computation.19 | async-start | bytes 4718592 | tf_op jit(solution)/shard_map/all_gather | solution.py:86
  83.7 85.9 %reduce-scatter.5.cloned.1.call-start = ((), (), s32[]{:S(2)}) async-start(), calls=%async_computation.23 | async-start | bytes 2359296 | tf_op jit(solution)/shard_map/reduce_scatter | solution.py:250
  143.2 28.5 %copy-start.18 = (f32[1,1,384,1024]{3,2,1,0:T(8,128)S(1)}, f32[1,1,384,1024]{3,2,1,0:T(8,128)}, u32[]{:S(2)}) copy-start(f32[1,1,384,1024]{3,2,1,0:T(8,128)} %param.27) | copy-start | bytes 4718596
  185.6 25.9 %all-to-all-start.6 = ((bf16[8,2,24576]{2,1,0:T(2,128)(2,1)}), bf16[8,2,24576]{2,1,0:T(2,128)(2,1)}, u32[]{:S(2)}, u32[]{:S(2)}) async-start(bf16[8,2,24576]{2,1,0:T(2,128)(2,1)} %reshape.592), calls=%async_computation.8 | async-start | bytes 1572864 | tf_op jit(solution)/shard_map/all_to_all | solution.py:143
  197.6 19.0 %copy-start.25 = (s32[1,4]{1,0:T(1,128)S(1)}, s32[1,4]{1,0:T(1,128)}, u32[]{:S(2)}) copy-start(s32[1,4]{1,0:T(1,128)} %param.25) | copy-start | bytes 52
  211.5 24.4 %all-to-all-start.15 = ((bf16[8,2,24576]{2,1,0:T(2,128)(2,1)}), bf16[8,2,24576]{2,1,0:T(2,128)(2,1)S(1)}, u32[]{:S(2)}, u32[]{:S(2)}) async-start(bf16[8,2,24576]{2,1,0:T(2,128)(2,1)} %reshape.612), calls=%async_computation.17 | async-start | bytes 1572864 | tf_op jit(solution)/shard_map/all_to_all | solution.py:176
  215.9 57.5 %all-gather.7.cloned.1.call-start = ((), (), s32[]{:S(2)}) async-start(), calls=%async_computation.20 | async-start | bytes 2359296 | tf_op jit(solution)/shard_map/all_gather | solution.py:87
  235.9 25.2 %all-to-all-start.11 = ((bf16[8,2,24576]{2,1,0:T(2,128)(2,1)}), bf16[8,2,24576]{2,1,0:T(2,128)(2,1)}, u32[]{:S(2)}, u32[]{:S(2)}) async-start(bf16[8,2,24576]{2,1,0:T(2,128)(2,1)} %reshape.604), calls=%async_computation.13 | async-start | bytes 1572864 | tf_op jit(solution)/shard_map/all_to_all | solution.py:170
  261.1 28.0 %all-to-all-start.7 = ((bf16[8,2,24576]{2,1,0:T(2,128)(2,1)}), bf16[8,2,24576]{2,1,0:T(2,128)(2,1)}, u32[]{:S(2)}, u32[]{:S(2)}) async-start(bf16[8,2,24576]{2,1,0:T(2,128)(2,1)} %reshape.594), calls=%async_computation.9 | async-start | bytes 1572864 | tf_op jit(solution)/shard_map/all_to_all | solution.py:157
  266.1 78.6 %reduce-scatter.3.cloned.1.call-start = ((), (), s32[]{:S(2)}) async-start(), calls=%async_computation.21 | async-start | bytes 4718592 | tf_op jit(solution)/shard_map/reduce_scatter | solution.py:247
  289.1 25.1 %all-to-all-start.12 = ((bf16[8,2,24576]{2,1,0:T(2,128)(2,1)}), bf16[8,2,24576]{2,1,0:T(2,128)(2,1)S(1)}, u32[]{:S(2)}, u32[]{:S(2)}) async-start(bf16[8,2,24576]{2,1,0:T(2,128)(2,1)} %reshape.606), calls=%async_computation.14 | async-start | bytes 1572864 | tf_op jit(solution)/shard_map/all_to_all | solution.py:183
  295.5 23.2 %copy-start.20 = (bf16[576,384]{1,0:T(8,128)(2,1)S(1)}, bf16[576,384]{1,0:T(8,128)(2,1)}, u32[]{:S(2)}) copy-start(bf16[576,384]{1,0:T(8,128)(2,1)} %copy-done.19) | copy-start | bytes 1327108
  314.2 8.6 %copy-start.14 = (bf16[8,2,24576]{2,1,0:T(2,128)(2,1)}, bf16[8,2,24576]{2,1,0:T(2,128)(2,1)S(1)}, u32[]{:S(2)}) copy-start(bf16[8,2,24576]{2,1,0:T(2,128)(2,1)S(1)} %all-to-all-done.12) | copy-start | bytes 2359300
  314.2 24.4 %all-to-all-start.16 = ((bf16[8,2,24576]{2,1,0:T(2,128)(2,1)}), bf16[8,2,24576]{2,1,0:T(2,128)(2,1)S(1)}, u32[]{:S(2)}, u32[]{:S(2)}) async-start(bf16[8,2,24576]{2,1,0:T(2,128)(2,1)} %reshape.614), calls=%async_computation.18 | async-start | bytes 1572864 | tf_op jit(solution)/shard_map/all_to_all | solution.py:185
  339.6 59.0 %all-to-all-start.1 = ((bf16[8,72,2048]{2,1,0:T(8,128)(2,1)}), bf16[8,72,2048]{2,1,0:T(8,128)(2,1)}, u32[]{:S(2)}, u32[]{:S(2)}) async-start(bf16[8,72,2048]{2,1,0:T(8,128)(2,1)} %bitcast.181), calls=%async_computation.1 | async-start | bytes 4718592 | tf_op jit(solution)/shard_map/all_to_all | solution.py:114
  398.6 42.3 %all-to-all-start.4 = ((bf16[8,2,49152]{2,1,0:T(2,128)(2,1)}), bf16[8,2,49152]{2,1,0:T(2,128)(2,1)}, u32[]{:S(2)}, u32[]{:S(2)}) async-start(bf16[8,2,49152]{2,1,0:T(2,128)(2,1)} %reshape.596), calls=%async_computation.5 | async-start | bytes 3145728 | tf_op jit(solution)/shard_map/all_to_all | solution.py:136
  440.9 41.5 %all-to-all-start.13 = ((bf16[8,2,49152]{2,1,0:T(2,128)(2,1)}), bf16[8,2,49152]{2,1,0:T(2,128)(2,1)S(1)}, u32[]{:S(2)}, u32[]{:S(2)}) async-start(bf16[8,2,49152]{2,1,0:T(2,128)(2,1)} %reshape.608), calls=%async_computation.15 | async-start | bytes 3145728 | tf_op jit(solution)/shard_map/all_to_all | solution.py:173
  463.4 26.0 %copy-start.23 = (s32[1,128,2]{1,2,0:T(2,128)S(1)}, s32[1,128,2]{1,2,0:T(2,128)}, u32[]{:S(2)}) copy-start(s32[1,128,2]{1,2,0:T(2,128)} %param.23) | copy-start | bytes 3076
  483.5 45.5 %all-to-all-start.9 = ((bf16[8,2,49152]{2,1,0:T(2,128)(2,1)}), bf16[8,2,49152]{2,1,0:T(2,128)(2,1)}, u32[]{:S(2)}, u32[]{:S(2)}) async-start(bf16[8,2,49152]{2,1,0:T(2,128)(2,1)} %reshape.600), calls=%async_computation.11 | async-start | bytes 3145728 | tf_op jit(solution)/shard_map/all_to_all | solution.py:167
  502.1 13.8 %copy-start.21 = (f32[1,2048]{1,0:T(1,128)S(1)}, f32[1,2048]{1,0:T(1,128)}, u32[]{:S(2)}) copy-start(f32[1,2048]{1,0:T(1,128)} %param.20) | copy-start | bytes 24580
  502.2 13.5 %collective-permute-start = (bf16[128,2048]{1,0:T(8,128)(2,1)S(1)}, bf16[128,2048]{1,0:T(8,128)(2,1)S(1)}, u32[]{:S(2)}, u32[]{:S(2)}) collective-permute-start(bf16[128,2048]{1,0:T(8,128)(2,1)S(1)} %fusion.30), channel_id=1, source_target_pairs={{16,0},{0,16},{17,1},{1,17},{18,2},{2,18},{19,3},{3,19},{20,4},{4,... | collective-permute-start | bytes 1572872 | tf_op jit(solution)/shard_map/ppermute | solution.py:26
  532.0 59.6 %all-to-all-start.2 = ((bf16[8,72,2048]{2,1,0:T(8,128)(2,1)}), bf16[8,72,2048]{2,1,0:T(8,128)(2,1)}, u32[]{:S(2)}, u32[]{:S(2)}) async-start(bf16[8,72,2048]{2,1,0:T(8,128)(2,1)} %bitcast.20), calls=%async_computation.2 | async-start | bytes 4718592 | tf_op jit(solution)/shard_map/all_to_all | solution.py:101
  591.6 41.3 %all-to-all-start.5 = ((bf16[8,2,49152]{2,1,0:T(2,128)(2,1)}), bf16[8,2,49152]{2,1,0:T(2,128)(2,1)S(1)}, u32[]{:S(2)}, u32[]{:S(2)}) async-start(bf16[8,2,49152]{2,1,0:T(2,128)(2,1)} %reshape.598), calls=%async_computation.6 | async-start | bytes 3145728 | tf_op jit(solution)/shard_map/all_to_all | solution.py:154
  634.1 42.1 %all-to-all-start.10 = ((bf16[8,2,49152]{2,1,0:T(2,128)(2,1)}), bf16[8,2,49152]{2,1,0:T(2,128)(2,1)}, u32[]{:S(2)}, u32[]{:S(2)}) async-start(bf16[8,2,49152]{2,1,0:T(2,128)(2,1)} %reshape.602), calls=%async_computation.12 | async-start | bytes 3145728 | tf_op jit(solution)/shard_map/all_to_all | solution.py:182
  639.2 63.7 %all-gather.9.cloned.1.call-start = ((), (), s32[]{:S(2)}) async-start(), calls=%async_computation.22 | async-start | bytes 4718592 | tf_op jit(solution)/shard_map/all_gather | solution.py:86
  676.2 62.6 %all-to-all-start.14 = ((bf16[8,2,49152]{2,1,0:T(2,128)(2,1)}), bf16[8,2,49152]{2,1,0:T(2,128)(2,1)S(1)}, u32[]{:S(2)}, u32[]{:S(2)}) async-start(bf16[8,2,49152]{2,1,0:T(2,128)(2,1)} %reshape.610), calls=%async_computation.16 | async-start | bytes 3145728 | tf_op jit(solution)/shard_map/all_to_all | solution.py:184
  680.6 51.5 %all-gather.11.cloned.1.call-start = ((), (), s32[]{:S(2)}) async-start(), calls=%async_computation.24 | async-start | bytes 2359296 | tf_op jit(solution)/shard_map/all_gather | solution.py:87
  739.9 63.1 %all-to-all-start.8 = ((bf16[8,72,2048]{2,1,0:T(8,128)(2,1)}), bf16[8,72,2048]{2,1,0:T(8,128)(2,1)}, u32[]{:S(2)}, u32[]{:S(2)}) async-start(bf16[8,72,2048]{2,1,0:T(8,128)(2,1)} %bitcast.180), calls=%async_computation.10 | async-start | bytes 4718592 | tf_op jit(solution)/shard_map/all_to_all | solution.py:114
  755.0 8.0 copy-start.2
  (22 other events, 73.3 us)
Sparse Core Ops, SparseCore 0:
  85.2 45.5 all-gather.4
  143.4 26.1 reduce-scatter.4
  218.8 26.8 all-gather.6
  286.3 43.1 reduce-scatter.2
  658.3 44.5 all-gather.8
  704.9 27.1 all-gather.10
where the time goes:
time: 828 us; the launch traced here: 822 us
  waiting for transfers between devices  369 us (45%)
  local copies, waits for them, and re-layouts  155 us (19%)
  other arithmetic  151 us (18%)
  starting transfers between devices  90.6 us (11%)
  matrix products  41.5 us (5%)
  between operations  15.1 us (2%)
    unnamed x90, local copies, waits for them, and re-layouts  88.9 us
    all_to_all x2, waiting for transfers between devices, forward_layer(): lax.all_to_all(send_rows, 'expert', split_axis=0, concat_axis=0, tiled=True)  80 us
    all_gather x2, waiting for transfers between devices, gather_weights(): lax.all_gather(inner_master.astype(jnp.bfloat16), 'dp', axis=3, tiled=True)  57 us
    all_to_all x1, waiting for transfers between devices, relocate_master(): lax.all_to_all(for_sending(inner_order), 'expert', split_axis=0, concat_a...  27.7 us
    reduce_scatter x1, waiting for transfers between devices, per_device(): lax.psum_scatter(grad_outer[None, None].astype(jnp.bfloat16), 'dp', scatt...  26.3 us
    all_gather x2, waiting for transfers between devices, gather_weights(): lax.all_gather(outer_master.astype(jnp.bfloat16), 'dp', axis=3, tiled=True)  25.7 us
    all_to_all x2, waiting for transfers between devices, forward_layer(): lax.all_to_all(half_out, 'expert', split_axis=0, concat_axis=0, tiled=True)  24.2 us
    all_to_all x1, waiting for transfers between devices, relocate_master(): lax.all_to_all(inner_master.reshape(devices, -1).astype(jnp.bfloat16), 'e...  19.2 us
  transfers between devices with their start and end apart: 24, of which 17 were waited for; matrix products, arithmetic and copies ran while one was open for 34% of the time, Pallas kernels for 0%

commit v1 on v0

v1 whole, which is shorter than its diff:
```python
import jax
import jax.numpy as jnp
from jax import lax
from jax.sharding import PartitionSpec as P

norm_eps = 1e-06
learn_rate = 0.001
beta_one = 0.9
beta_two = 0.95
adam_eps = 1e-08
bias_one = 0.999973438601112
bias_two = 0.994079470779667


def for_sending(array):

    def short(part):
        return part.astype(jnp.bfloat16) if part.dtype == jnp.float32 else part

    return jax.tree.map(short, array)


def passed_along(block, axis, distance):
    devices = range(lax.axis_size(axis))
    route = [((i - distance) % len(devices), i) for i in devices]
    return lax.ppermute(block, axis, route)


def normed(values, gain_row):
    widened = values.astype(jnp.float32)
    inverse_rms = lax.rsqrt(jnp.mean(widened * widened, axis=-1, keepdims=True) + norm_eps)
    return (widened * inverse_rms * gain_row).astype(jnp.bfloat16)


def silu_parts(gate_proj):
    logistic = jax.nn.sigmoid(gate_proj)
    return (gate_proj * logistic, logistic * (1.0 + gate_proj * (1.0 - logistic)))


def half_forward(token_rows, inner_full, outer_full):
    gate_proj = jnp.dot(token_rows, inner_full[0], preferred_element_type=jnp.float32)
    up_proj = jnp.dot(token_rows, inner_full[1], preferred_element_type=jnp.float32)
    activity = (silu_parts(gate_proj)[0] * up_proj).astype(jnp.bfloat16)
    half_out = jnp.dot(activity, outer_full, preferred_element_type=jnp.float32).astype(
        jnp.bfloat16
    )
    return (half_out, activity, gate_proj, up_proj)


def half_backward(token_rows, grad_rows, outer_full, activity, gate_proj, up_proj):
    grad_outer = jnp.dot(activity.T, grad_rows, preferred_element_type=jnp.float32)
    d_active = jnp.dot(grad_rows, outer_full.T, preferred_element_type=jnp.float32)
    swish_value, swish_slope = silu_parts(gate_proj)
    d_gate = (d_active * up_proj * swish_slope).astype(jnp.bfloat16)
    d_upper = (d_active * swish_value).astype(jnp.bfloat16)
    grad_gate = jnp.dot(token_rows.T, d_gate, preferred_element_type=jnp.float32)
    grad_upper = jnp.dot(token_rows.T, d_upper, preferred_element_type=jnp.float32)
    return (jnp.stack([grad_gate, grad_upper]), grad_outer)


def slot_index(ids, pair_of, capacity):
    flattened = ids.reshape(-1)
    expert_row = jnp.arange(pair_of.shape[0], dtype=jnp.int32)
    onehot = (flattened[:, None] == expert_row[None, :]).astype(jnp.int32)
    ranking = jnp.sum((jnp.cumsum(onehot, axis=0) - 1) * onehot, axis=1)
    target = jnp.sum(onehot * pair_of[None, :], axis=1)
    return (target * capacity + ranking).reshape(ids.shape)


def selection(slots, values, total_slots):
    positions = jnp.arange(total_slots, dtype=jnp.int32)
    result = jnp.zeros((total_slots, slots.shape[0]), jnp.float32)
    for column in range(slots.shape[1]):
        result = result + jnp.where(
            slots[:, column][None, :] == positions[:, None], values[:, column][None, :], 0.0
        )
    return result


def across_chips(blocks):
    pairs = blocks.shape[0]
    groups = [[2 * pair + core for pair in range(pairs)] for core in range(2)]
    return lax.all_to_all(
        blocks, "expert", split_axis=0, concat_axis=0, tiled=True, axis_index_groups=groups
    )


def to_partner(block):
    devices = range(lax.axis_size("expert"))
    return lax.ppermute(block, "expert", [(i, i ^ 1) for i in devices])


def dispatched(packed, pair_count, capacity):
    own = across_chips(packed.reshape(pair_count, capacity, packed.shape[-1]))
    own = own.reshape(pair_count * capacity, -1)
    return jnp.concatenate([own, to_partner(own)], axis=0)


def gather_weights(inner_master, outer_master):
    inner_full, outer_full = (
        lax.all_gather(inner_master.astype(jnp.bfloat16), "dp", axis=3, tiled=True),
        lax.all_gather(outer_master.astype(jnp.bfloat16), "dp", axis=3, tiled=True),
    )
    return (inner_full[0, 0], outer_full[0, 0])


def pack_rows(token_rows, gain_row, ids, pair_of, capacity):
    pair_count = pair_of.shape[0]
    normal = normed(token_rows, gain_row)
    slots = slot_index(ids, pair_of, capacity)
    picker = selection(slots, jnp.ones(slots.shape, jnp.float32), pair_count * capacity).astype(
        jnp.bfloat16
    )
    packed = jnp.dot(picker, normal, preferred_element_type=jnp.float32).astype(jnp.bfloat16)
    return (slots, dispatched(packed, pair_count, capacity))


def returned_rows(token_rows, half_out, slots, gates, pair_count, capacity):
    rows = pair_count * capacity
    summed = half_out[:rows].astype(jnp.float32) + to_partner(half_out[rows:]).astype(jnp.float32)
    back = across_chips(summed.astype(jnp.bfloat16).reshape(pair_count, capacity, -1))
    weighting = selection(slots, gates, rows)
    mixed = lax.dot_general(
        weighting,
        back.reshape(rows, -1).astype(jnp.float32),
        (((0,), (0,)), ((), ())),
        precision=lax.Precision.HIGHEST,
    )
    return (token_rows.astype(jnp.float32) + mixed).astype(jnp.bfloat16)


def adam_step(weight, mean, square, grads):
    mean_new = (beta_one * mean.astype(jnp.float32) + (1.0 - beta_one) * grads).astype(jnp.bfloat16)
    square_new = (beta_two * square.astype(jnp.float32) + (1.0 - beta_two) * grads * grads).astype(
        jnp.bfloat16
    )
    mean_wide = lax.optimization_barrier(mean_new).astype(jnp.float32)
    square_wide = lax.optimization_barrier(square_new).astype(jnp.float32)
    update = mean_wide / bias_one / (jnp.sqrt(square_wide / bias_two) + adam_eps)
    return (weight - learn_rate * update, mean_new, square_new)


def relocated(inner, outer, source):
    devices = source.shape[0]

    def moved(parts):
        spread = lax.all_to_all(parts, "expert", split_axis=0, concat_axis=0, tiled=True)
        ordered = jnp.take(spread, source, axis=0)
        return lax.all_to_all(ordered, "expert", split_axis=0, concat_axis=0, tiled=True)

    two, rows, columns = inner.shape[2:]
    parts = inner.reshape(two, devices, rows // devices, columns).transpose(1, 0, 2, 3)
    inner_back = moved(parts).transpose(1, 0, 2, 3).reshape(inner.shape)
    parts = outer.reshape(devices, outer.shape[2] // devices, outer.shape[3])
    return (inner_back, moved(parts).reshape(outer.shape))


def per_device(
    tokens,
    cotangent,
    norm_gain,
    first_ids,
    first_gates,
    second_ids,
    second_gates,
    new_slot,
    inner_weight,
    outer_weight,
    inner_mean,
    outer_mean,
    inner_square,
    outer_square,
):
    pair_count = new_slot.shape[1]
    rows_here = tokens.shape[1]
    top_count = first_ids.shape[2]
    width = tokens.shape[2]
    usual = rows_here * top_count // pair_count
    capacity = min(rows_here, usual + usual // 8)
    gain_row = norm_gain[0]
    identity_map = jnp.arange(pair_count, dtype=jnp.int32)
    new_pairs = new_slot[0]
    inverse = jnp.sum(
        jnp.where(new_pairs[:, None] == identity_map[None, :], identity_map[:, None], 0), axis=0
    )
    device_ids = jnp.arange(2 * pair_count, dtype=jnp.int32)
    source = 2 * jnp.repeat(inverse, 2) + device_ids % 2
    inner_low, outer_low = relocated(*for_sending((inner_weight, outer_weight)), source)
    inner_full, outer_full = gather_weights(inner_low, outer_low)
    slots, arrived = pack_rows(tokens[0], gain_row, first_ids[0], new_pairs, capacity)
    weighting = selection(slots, first_gates[0], pair_count * capacity)
    grad_packed = jnp.dot(
        weighting, cotangent[0].astype(jnp.float32), precision=lax.Precision.HIGHEST
    ).astype(jnp.bfloat16)
    grad_arrived = dispatched(grad_packed, pair_count, capacity)
    moments = (inner_mean, outer_mean, inner_square, outer_square)
    moments, inner_low, outer_low = lax.optimization_barrier((moments, inner_low, outer_low))
    old_mean_in, old_mean_out = relocated(moments[0], moments[1], source)
    old_square_in, old_square_out = relocated(moments[2], moments[3], source)
    half_out, activity, gate_proj, up_proj = half_forward(arrived, inner_full, outer_full)
    grad_inner, grad_outer = half_backward(
        arrived, grad_arrived, outer_full, activity, gate_proj, up_proj
    )
    sum_inner, sum_outer = (
        lax.psum_scatter(
            grad_inner[None, None].astype(jnp.bfloat16), "dp", scatter_dimension=3, tiled=True
        ).astype(jnp.float32),
        lax.psum_scatter(
            grad_outer[None, None].astype(jnp.bfloat16), "dp", scatter_dimension=3, tiled=True
        ).astype(jnp.float32),
    )
    first_out = returned_rows(
        tokens[0], half_out, slots, first_gates[0], pair_count, capacity
    )
    moved_inner, moved_mean_in, moved_square_in = adam_step(
        inner_low.astype(jnp.float32), old_mean_in, old_square_in, sum_inner
    )
    moved_outer, moved_mean_out, moved_square_out = adam_step(
        outer_low.astype(jnp.float32), old_mean_out, old_square_out, sum_outer
    )
    inner_two, outer_two = gather_weights(moved_inner, moved_outer)
    shifted = passed_along(first_out, "pipe", 1)
    slots_two, arrived_two = pack_rows(shifted, gain_row, second_ids[0], new_pairs, capacity)
    half_two = half_forward(arrived_two, inner_two, outer_two)[0]
    second_out = returned_rows(
        shifted, half_two, slots_two, second_gates[0], pair_count, capacity
    )
    return (
        second_out[None],
        moved_inner,
        moved_outer,
        moved_mean_in,
        moved_mean_out,
        moved_square_in,
        moved_square_out,
    )


def solution(mesh):
    return jax.shard_map(
        per_device,
        mesh=mesh,
        in_specs=(
            P("pipe", ("expert", "dp"), None),
            P("pipe", ("expert", "dp"), None),
            P("pipe", None),
            P("pipe", ("expert", "dp"), None),
            P("pipe", ("expert", "dp"), None),
            P("pipe", ("expert", "dp"), None),
            P("pipe", ("expert", "dp"), None),
            P("pipe", None),
            P("pipe", "expert", None, "dp", None),
            P("pipe", "expert", None, "dp"),
            P("pipe", "expert", None, "dp", None),
            P("pipe", "expert", None, "dp"),
            P("pipe", "expert", None, "dp", None),
            P("pipe", "expert", None, "dp"),
        ),
        out_specs=(
            P("pipe", ("expert", "dp"), None),
            P("pipe", "expert", None, "dp", None),
            P("pipe", "expert", None, "dp"),
            P("pipe", "expert", None, "dp", None),
            P("pipe", "expert", None, "dp"),
            P("pipe", "expert", None, "dp", None),
            P("pipe", "expert", None, "dp"),
        ),
        check_vma=False,
    )
```

time: 828 us -> 601 us (0.73)
  local copies, waits for them, and re-layouts: 155 us -> 28.6 us
  other arithmetic: 151 us -> 39.1 us
  blocking collectives: 0 us -> 40.1 us
  waiting for transfers between devices: 369 us -> 354 us
  starting transfers between devices: 90.6 us -> 77.1 us
    all_to_all x16 -> x0, other arithmetic: 93.9 us -> none  [the longest x3 16 us: relocate_moments(): lax.all_to_all(ordered[2], 'expert', split_axis=0, concat_axis=0, tiled=T...]
    all_to_all x17 -> x16, waiting for transfers between devices: 248 us -> 333 us  [the longest x6 125 us: moved(): lax.all_to_all(parts, 'expert', split_axis=0, concat_axis=0, tiled=True)]
    unnamed x90 -> x74, local copies, waits for them, and re-layouts: 88.9 us -> 5.74 us
    all_gather x2, waiting for transfers between devices: 57 us -> 0.02 us  [gather_weights(): lax.all_gather(inner_master.astype(jnp.bfloat16), 'dp', axis=3, tiled=True)]
    all_to_all x0 -> x1, blocking collectives: none -> 40.1 us  [moved(): lax.all_to_all(ordered, 'expert', split_axis=0, concat_axis=0, tiled=True)]
    reduce_scatter x1, waiting for transfers between devices: 26.3 us -> 0.02 us  [per_device(): lax.psum_scatter(grad_outer[None, None].astype(jnp.bfloat16), 'dp', scatt...]
    all_gather x2, waiting for transfers between devices: 25.7 us -> 0.01 us  [gather_weights(): lax.all_gather(outer_master.astype(jnp.bfloat16), 'dp', axis=3, tiled=True)]
    convert_element_type x6 -> x2, other arithmetic: 25.3 us -> 4.64 us  [returned_rows(): summed.astype(jnp.bfloat16).reshape(pair_count, capacity, -1)]
  transfers between devices with their start and end apart: 24 -> 28, of which waited for: 17 -> 20; matrix products, arithmetic and copies ran while one was open for 34% -> 16% of each run, Pallas kernels for 0% -> 0%
where the time goes in v1:
time: 601 us; the launch traced here: 598 us
  waiting for transfers between devices  354 us (59%)
  starting transfers between devices  77.1 us (13%)
  matrix products  44.5 us (7%)
  blocking collectives  40.1 us (7%)
  other arithmetic  39.1 us (7%)
  local copies, waits for them, and re-layouts  28.6 us (5%)
  between operations  14.6 us (2%)
    all_to_all x6, waiting for transfers between devices, moved(): lax.all_to_all(parts, 'expert', split_axis=0, concat_axis=0, tiled=True)  125 us
    all_to_all x5, waiting for transfers between devices, across_chips(): lax.all_to_all(blocks, 'expert', split_axis=0, concat_axis=0, tiled=True,...  119 us
    all_to_all x5, waiting for transfers between devices, moved(): lax.all_to_all(ordered, 'expert', split_axis=0, concat_axis=0, tiled=True)  89.1 us
    all_to_all x1, blocking collectives, moved(): lax.all_to_all(ordered, 'expert', split_axis=0, concat_axis=0, tiled=True)  40.1 us
    all_to_all x6, starting transfers between devices, moved(): lax.all_to_all(parts, 'expert', split_axis=0, concat_axis=0, tiled=True)  29.7 us
    all_to_all x5, starting transfers between devices, moved(): lax.all_to_all(ordered, 'expert', split_axis=0, concat_axis=0, tiled=True)  23.3 us
    all_to_all x5, starting transfers between devices, across_chips(): lax.all_to_all(blocks, 'expert', split_axis=0, concat_axis=0, tiled=True,...  20.1 us
    gather x6, local copies, waits for them, and re-layouts, moved(): ordered = jnp.take(spread, source, axis=0)  12.4 us
  transfers between devices with their start and end apart: 28, of which 20 were waited for; matrix products, arithmetic and copies ran while one was open for 16% of the time, Pallas kernels for 0%

profile of v1, /device:TPU:1, one launch (start us, length us, event | category | flops | bytes accessed | tf_op | source)
XLA Modules:
  0.0 598.2 jit_solution(6299541725678960014)
XLA Ops:
  9.7 6.5 %all-to-all-start.3 = ((bf16[8,48,1024]{2,1,0:T(8,128)(2,1)}), bf16[8,48,1024]{2,1,0:T(8,128)(2,1)S(1)}, u32[]{:S(2)}, u32[]{:S(2)}) async-start(bf16[8,48,1024]{2,1,0:T(8,128)(2,1)} %bitcast.17), calls=%async_computation.3 | async-start | bytes 1572864 | tf_op jit(solution)/shard_map/all_to_all | solution.py:147
  22.4 13.7 %all-to-all-done.3 = bf16[8,48,1024]{2,1,0:T(8,128)(2,1)S(1)} async-done(((bf16[8,48,1024]{2,1,0:T(8,128)(2,1)}), bf16[8,48,1024]{2,1,0:T(8,128)(2,1)S(1)}, u32[]{:S(2)}, u32[]{:S(2)}) %all-to-all-start.3) | async-done | bytes 786464 | tf_op jit(solution)/shard_map/all_to_all | solution.py:147
  43.1 24.7 %all-to-all-done = bf16[4,72,2048]{2,1,0:T(8,128)(2,1)S(1)} async-done(((bf16[4,72,2048]{2,1,0:T(8,128)(2,1)}), bf16[4,72,2048]{2,1,0:T(8,128)(2,1)S(1)}, u32[]{:S(2)}, u32[]{:S(2)}) %all-to-all-start) | async-done | bytes 1179680 | tf_op jit(solution)/shard_map/all_to_all | solution.py:83
  68.8 4.9 all-to-all-start.1
  77.6 33.0 %all-to-all-done.1 = bf16[8,2,128,384]{3,2,1,0:T(8,128)(2,1)S(1)} async-done(((bf16[8,2,128,384]{3,2,1,0:T(8,128)(2,1)}), bf16[8,2,128,384]{3,2,1,0:T(8,128)(2,1)S(1)}, u32[]{:S(2)}, u32[]{:S(2)}) %all-to-all-start.1) | async-done | bytes 1572896 | tf_op jit(solution)/shard_map/all_to_all | solution.py:147
  110.5 4.4 all-to-all-start.4
  119.6 15.3 %all-to-all-done.4 = bf16[8,48,1024]{2,1,0:T(8,128)(2,1)S(1)} async-done(((bf16[8,48,1024]{2,1,0:T(8,128)(2,1)}), bf16[8,48,1024]{2,1,0:T(8,128)(2,1)S(1)}, u32[]{:S(2)}, u32[]{:S(2)}) %all-to-all-start.4) | async-done | bytes 786464 | tf_op jit(solution)/shard_map/all_to_all | solution.py:149
  135.8 4.4 all-to-all-start.2
  142.4 34.8 %all-to-all-done.2 = bf16[8,2,128,384]{3,2,1,0:T(8,128)(2,1)S(1)} async-done(((bf16[8,2,128,384]{3,2,1,0:T(8,128)(2,1)}), bf16[8,2,128,384]{3,2,1,0:T(8,128)(2,1)S(1)}, u32[]{:S(2)}, u32[]{:S(2)}) %all-to-all-start.2) | async-done | bytes 1572896 | tf_op jit(solution)/shard_map/all_to_all | solution.py:149
  182.8 26.8 %all-to-all-done.9 = bf16[4,72,2048]{2,1,0:T(8,128)(2,1)} async-done(((bf16[4,72,2048]{2,1,0:T(8,128)(2,1)}), bf16[4,72,2048]{2,1,0:T(8,128)(2,1)}, u32[]{:S(2)}, u32[]{:S(2)}) %all-to-all-start.9) | async-done | bytes 1179680 | tf_op jit(solution)/shard_map/all_to_all | solution.py:83
  209.6 4.8 all-to-all-start.14
  215.2 19.3 %all-to-all-done.14 = bf16[8,48,1024]{2,1,0:T(8,128)(2,1)S(1)} async-done(((bf16[8,48,1024]{2,1,0:T(8,128)(2,1)}), bf16[8,48,1024]{2,1,0:T(8,128)(2,1)S(1)}, u32[]{:S(2)}, u32[]{:S(2)}) %all-to-all-start.14) | async-done | bytes 786464 | tf_op jit(solution)/shard_map/all_to_all | solution.py:147
  234.4 4.5 all-to-all-start.12
  241.1 17.9 %all-to-all-done.12 = bf16[8,48,1024]{2,1,0:T(8,128)(2,1)S(1)} async-done(((bf16[8,48,1024]{2,1,0:T(8,128)(2,1)}), bf16[8,48,1024]{2,1,0:T(8,128)(2,1)S(1)}, u32[]{:S(2)}, u32[]{:S(2)}) %all-to-all-start.12) | async-done | bytes 786464 | tf_op jit(solution)/shard_map/all_to_all | solution.py:147
  259.9 4.4 all-to-all-start.7
  267.5 4.4 fusion.19
  273.3 27.9 %all-to-all-done.7 = bf16[8,2,128,384]{3,2,1,0:T(8,128)(2,1)S(1)} async-done(((bf16[8,2,128,384]{3,2,1,0:T(8,128)(2,1)}), bf16[8,2,128,384]{3,2,1,0:T(8,128)(2,1)S(1)}, u32[]{:S(2)}, u32[]{:S(2)}) %all-to-all-start.7) | async-done | bytes 1572896 | tf_op jit(solution)/shard_map/all_to_all | solution.py:147
  301.2 4.4 all-to-all-start.10
  329.1 13.4 %all-to-all-done.10 = bf16[8,2,128,384]{3,2,1,0:T(8,128)(2,1)S(1)} async-done(((bf16[8,2,128,384]{3,2,1,0:T(8,128)(2,1)}), bf16[8,2,128,384]{3,2,1,0:T(8,128)(2,1)S(1)}, u32[]{:S(2)}, u32[]{:S(2)}) %all-to-all-start.10) | async-done | bytes 1572896 | tf_op jit(solution)/shard_map/all_to_all | solution.py:147
  342.5 5.1 all-to-all-start.13
  354.8 12.9 %all-to-all-done.13 = bf16[8,48,1024]{2,1,0:T(8,128)(2,1)} async-done(((bf16[8,48,1024]{2,1,0:T(8,128)(2,1)}), bf16[8,48,1024]{2,1,0:T(8,128)(2,1)}, u32[]{:S(2)}, u32[]{:S(2)}) %all-to-all-start.13) | async-done | bytes 786464 | tf_op jit(solution)/shard_map/all_to_all | solution.py:149
  367.7 40.1 %all_to_all.85 = bf16[8,2,128,384]{3,2,1,0:T(8,128)(2,1)S(1)} all-to-all(bf16[8,2,128,384]{3,2,1,0:T(8,128)(2,1)S(1)} %get-tuple-element.45), channel_id=1, replica_groups=mesh['pipe'=2,'expert'=8,'dp'=2] {'expert'}, dimensions={0} | all-to-all | bytes 3145728 | tf_op jit(solution)/shard_map/all_to_all | solution.py:149
  407.8 4.5 all-to-all-start.11
  425.3 23.9 %all-to-all-done.11 = bf16[8,2,128,384]{3,2,1,0:T(8,128)(2,1)S(1)} async-done(((bf16[8,2,128,384]{3,2,1,0:T(8,128)(2,1)}), bf16[8,2,128,384]{3,2,1,0:T(8,128)(2,1)S(1)}, u32[]{:S(2)}, u32[]{:S(2)}) %all-to-all-start.11) | async-done | bytes 1572896 | tf_op jit(solution)/shard_map/all_to_all | solution.py:149
  449.2 4.3 all-to-all-start.5
  465.1 16.5 %all-to-all-done.5 = bf16[4,72,2048]{2,1,0:T(8,128)(2,1)} async-done(((bf16[4,72,2048]{2,1,0:T(8,128)(2,1)}), bf16[4,72,2048]{2,1,0:T(8,128)(2,1)}, u32[]{:S(2)}, u32[]{:S(2)}) %all-to-all-start.5) | async-done | bytes 1179680 | tf_op jit(solution)/shard_map/all_to_all | solution.py:83
  481.7 4.8 all-to-all-start.15
  490.4 12.0 %collective-permute-done.2 = bf16[128,2048]{1,0:T(8,128)(2,1)S(1)} collective-permute-done((bf16[128,2048]{1,0:T(8,128)(2,1)S(1)}, bf16[128,2048]{1,0:T(8,128)(2,1)S(1)}, u32[]{:S(2)}, u32[]{:S(2)}) %collective-permute-start.2) | collective-permute-done | bytes 524320 | tf_op jit(solution)/shard_map/ppermute | solution.py:26
  516.6 22.4 %all-to-all-done.6 = bf16[4,72,2048]{2,1,0:T(8,128)(2,1)} async-done(((bf16[4,72,2048]{2,1,0:T(8,128)(2,1)}), bf16[4,72,2048]{2,1,0:T(8,128)(2,1)}, u32[]{:S(2)}, u32[]{:S(2)}) %all-to-all-start.6) | async-done | bytes 1179680 | tf_op jit(solution)/shard_map/all_to_all | solution.py:83
  543.1 4.5 fusion.14
  547.6 5.5 convolution_convert_fusion
  561.3 28.2 %all-to-all-done.16 = bf16[4,72,2048]{2,1,0:T(8,128)(2,1)S(1)} async-done(((bf16[4,72,2048]{2,1,0:T(8,128)(2,1)}), bf16[4,72,2048]{2,1,0:T(8,128)(2,1)S(1)}, u32[]{:S(2)}, u32[]{:S(2)}) %all-to-all-start.16) | async-done | bytes 1179680 | tf_op jit(solution)/shard_map/all_to_all | solution.py:83
  (188 shorter events, 129.2 us)
Async XLA Ops:
  7.2 133.1 %copy-start = (bf16[1,128,2048]{2,1,0:T(8,128)(2,1)S(1)}, bf16[1,128,2048]{2,1,0:T(8,128)(2,1)}, u32[]{:S(2)}) copy-start(bf16[1,128,2048]{2,1,0:T(8,128)(2,1)} %param.19) | copy-start | bytes 1572868
  9.7 26.5 %all-to-all-start.3 = ((bf16[8,48,1024]{2,1,0:T(8,128)(2,1)}), bf16[8,48,1024]{2,1,0:T(8,128)(2,1)S(1)}, u32[]{:S(2)}, u32[]{:S(2)}) async-start(bf16[8,48,1024]{2,1,0:T(8,128)(2,1)} %bitcast.17), calls=%async_computation.3 | async-start | bytes 1572864 | tf_op jit(solution)/shard_map/all_to_all | solution.py:147
  36.2 31.6 %all-to-all-start = ((bf16[4,72,2048]{2,1,0:T(8,128)(2,1)}), bf16[4,72,2048]{2,1,0:T(8,128)(2,1)S(1)}, u32[]{:S(2)}, u32[]{:S(2)}) async-start(bf16[4,72,2048]{2,1,0:T(8,128)(2,1)} %bitcast.9), calls=%async_computation | async-start | bytes 2359296 | tf_op jit(solution)/shard_map/all_to_all | solution.py:83
  68.8 41.7 %all-to-all-start.1 = ((bf16[8,2,128,384]{3,2,1,0:T(8,128)(2,1)}), bf16[8,2,128,384]{3,2,1,0:T(8,128)(2,1)S(1)}, u32[]{:S(2)}, u32[]{:S(2)}) async-start(bf16[8,2,128,384]{3,2,1,0:T(8,128)(2,1)} %bitcast.126), calls=%async_computation.1 | async-start | bytes 3145728 | tf_op jit(solution)/shard_map/all_to_all | solution.py:147
  110.5 24.4 %all-to-all-start.4 = ((bf16[8,48,1024]{2,1,0:T(8,128)(2,1)}), bf16[8,48,1024]{2,1,0:T(8,128)(2,1)S(1)}, u32[]{:S(2)}, u32[]{:S(2)}) async-start(bf16[8,48,1024]{2,1,0:T(8,128)(2,1)} %broadcast_select_fusion.5), calls=%async_computation.4 | async-start | bytes 1572864 | tf_op jit(solution)/shard_map/all_to_all | solution.py:149
  135.8 41.3 %all-to-all-start.2 = ((bf16[8,2,128,384]{3,2,1,0:T(8,128)(2,1)}), bf16[8,2,128,384]{3,2,1,0:T(8,128)(2,1)S(1)}, u32[]{:S(2)}, u32[]{:S(2)}) async-start(bf16[8,2,128,384]{3,2,1,0:T(8,128)(2,1)} %broadcast_select_fusion.2), calls=%async_computation.2 | async-start | bytes 3145728 | tf_op jit(solution)/shard_map/all_to_all | solution.py:149
  177.1 32.4 %all-to-all-start.9 = ((bf16[4,72,2048]{2,1,0:T(8,128)(2,1)}), bf16[4,72,2048]{2,1,0:T(8,128)(2,1)}, u32[]{:S(2)}, u32[]{:S(2)}) async-start(bf16[4,72,2048]{2,1,0:T(8,128)(2,1)} %bitcast.139), calls=%async_computation.9 | async-start | bytes 2359296 | tf_op jit(solution)/shard_map/all_to_all | solution.py:83
  209.6 24.9 %all-to-all-start.14 = ((bf16[8,48,1024]{2,1,0:T(8,128)(2,1)}), bf16[8,48,1024]{2,1,0:T(8,128)(2,1)S(1)}, u32[]{:S(2)}, u32[]{:S(2)}) async-start(bf16[8,48,1024]{2,1,0:T(8,128)(2,1)} %bitcast.147), calls=%async_computation.16 | async-start | bytes 1572864 | tf_op jit(solution)/shard_map/all_to_all | solution.py:147
  214.4 53.1 %all-gather.7.cloned.1.call-start = ((), (), s32[]{:S(2)}) async-start(), calls=%async_computation.20 | async-start | bytes 2359296 | tf_op jit(solution)/shard_map/all_gather | solution.py:102
  234.4 24.6 %all-to-all-start.12 = ((bf16[8,48,1024]{2,1,0:T(8,128)(2,1)}), bf16[8,48,1024]{2,1,0:T(8,128)(2,1)S(1)}, u32[]{:S(2)}, u32[]{:S(2)}) async-start(bf16[8,48,1024]{2,1,0:T(8,128)(2,1)} %bitcast.148), calls=%async_computation.13 | async-start | bytes 1572864 | tf_op jit(solution)/shard_map/all_to_all | solution.py:147
  239.0 66.7 %all-gather.5.cloned.1.call-start = ((), (), s32[]{:S(2)}) async-start(), calls=%async_computation.19 | async-start | bytes 4718592 | tf_op jit(solution)/shard_map/all_gather | solution.py:101
  259.9 41.3 %all-to-all-start.7 = ((bf16[8,2,128,384]{3,2,1,0:T(8,128)(2,1)}), bf16[8,2,128,384]{3,2,1,0:T(8,128)(2,1)S(1)}, u32[]{:S(2)}, u32[]{:S(2)}) async-start(bf16[8,2,128,384]{3,2,1,0:T(8,128)(2,1)} %bitcast.125), calls=%async_computation.7 | async-start | bytes 3145728 | tf_op jit(solution)/shard_map/all_to_all | solution.py:147
  264.3 3.2 collective-permute-start.4
  264.5 41.1 %collective-permute-start = (bf16[288,2048]{1,0:T(8,128)(2,1)}, bf16[288,2048]{1,0:T(8,128)(2,1)}, u32[]{:S(2)}, u32[]{:S(2)}) collective-permute-start(bf16[288,2048]{1,0:T(8,128)(2,1)} %bitcast.142), channel_id=1, source_target_pairs={{0,2},{2,0},{4,6},{6,4},{8,10},{10,8},{12,14},{14,12},{1,3},{3,1},... | collective-permute-start | bytes 3538952 | tf_op jit(solution)/shard_map/ppermute | solution.py:90
  301.2 41.3 %all-to-all-start.10 = ((bf16[8,2,128,384]{3,2,1,0:T(8,128)(2,1)}), bf16[8,2,128,384]{3,2,1,0:T(8,128)(2,1)S(1)}, u32[]{:S(2)}, u32[]{:S(2)}) async-start(bf16[8,2,128,384]{3,2,1,0:T(8,128)(2,1)} %bitcast.124), calls=%async_computation.11 | async-start | bytes 3145728 | tf_op jit(solution)/shard_map/all_to_all | solution.py:147
  305.6 152.1 %reduce-scatter.3.cloned.1.call-start = ((), (), s32[]{:S(2)}) async-start(), calls=%async_computation.21 | async-start | bytes 4718592 | tf_op jit(solution)/shard_map/reduce_scatter | solution.py:205
  342.5 25.2 %all-to-all-start.13 = ((bf16[8,48,1024]{2,1,0:T(8,128)(2,1)}), bf16[8,48,1024]{2,1,0:T(8,128)(2,1)}, u32[]{:S(2)}, u32[]{:S(2)}) async-start(bf16[8,48,1024]{2,1,0:T(8,128)(2,1)} %get-tuple-element.47), calls=%async_computation.14 | async-start | bytes 1572864 | tf_op jit(solution)/shard_map/all_to_all | solution.py:149
  407.8 41.4 %all-to-all-start.11 = ((bf16[8,2,128,384]{3,2,1,0:T(8,128)(2,1)}), bf16[8,2,128,384]{3,2,1,0:T(8,128)(2,1)S(1)}, u32[]{:S(2)}, u32[]{:S(2)}) async-start(bf16[8,2,128,384]{3,2,1,0:T(8,128)(2,1)} %get-tuple-element.46), calls=%async_computation.12 | async-start | bytes 3145728 | tf_op jit(solution)/shard_map/all_to_all | solution.py:149
  412.3 100.2 %reduce-scatter.5.cloned.1.call-start = ((), (), s32[]{:S(2)}) async-start(), calls=%async_computation.23 | async-start | bytes 2359296 | tf_op jit(solution)/shard_map/reduce_scatter | solution.py:208
  417.8 4.4 collective-permute-start.1
  449.2 32.5 %all-to-all-start.5 = ((bf16[4,72,2048]{2,1,0:T(8,128)(2,1)}), bf16[4,72,2048]{2,1,0:T(8,128)(2,1)}, u32[]{:S(2)}, u32[]{:S(2)}) async-start(bf16[4,72,2048]{2,1,0:T(8,128)(2,1)} %bitcast.137), calls=%async_computation.5 | async-start | bytes 2359296 | tf_op jit(solution)/shard_map/all_to_all | solution.py:83
  453.5 89.5 %all-gather.9.cloned.1.call-start = ((), (), s32[]{:S(2)}) async-start(), calls=%async_computation.22 | async-start | bytes 4718592 | tf_op jit(solution)/shard_map/all_gather | solution.py:101
  465.1 21.4 %copy-start.10 = (bf16[1,128,2048]{2,1,0:T(8,128)(2,1)S(1)}, bf16[1,128,2048]{2,1,0:T(8,128)(2,1)}, u32[]{:S(2)}) copy-start(bf16[1,128,2048]{2,1,0:T(8,128)(2,1)} %param.18) | copy-start | bytes 1572868
  481.7 24.9 %all-to-all-start.15 = ((bf16[8,48,1024]{2,1,0:T(8,128)(2,1)}), bf16[8,48,1024]{2,1,0:T(8,128)(2,1)S(1)}, u32[]{:S(2)}, u32[]{:S(2)}) async-start(bf16[8,48,1024]{2,1,0:T(8,128)(2,1)} %get-tuple-element.48), calls=%async_computation.17 | async-start | bytes 1572864 | tf_op jit(solution)/shard_map/all_to_all | solution.py:149
  488.8 13.5 %collective-permute-start.2 = (bf16[128,2048]{1,0:T(8,128)(2,1)S(1)}, bf16[128,2048]{1,0:T(8,128)(2,1)S(1)}, u32[]{:S(2)}, u32[]{:S(2)}) collective-permute-start(bf16[128,2048]{1,0:T(8,128)(2,1)S(1)} %fusion.7), channel_id=1, source_target_pairs={{16,0},{0,16},{17,1},{1,17},{18,2},{2,18},{19,3},{3,19},{20,4},{4,... | collective-permute-start | bytes 1572872 | tf_op jit(solution)/shard_map/ppermute | solution.py:26
  506.5 32.4 %all-to-all-start.6 = ((bf16[4,72,2048]{2,1,0:T(8,128)(2,1)}), bf16[4,72,2048]{2,1,0:T(8,128)(2,1)}, u32[]{:S(2)}, u32[]{:S(2)}) async-start(bf16[4,72,2048]{2,1,0:T(8,128)(2,1)} %bitcast.27), calls=%async_computation.6 | async-start | bytes 2359296 | tf_op jit(solution)/shard_map/all_to_all | solution.py:83
  510.8 36.7 %all-gather.11.cloned.1.call-start = ((), (), s32[]{:S(2)}) async-start(), calls=%async_computation.24 | async-start | bytes 2359296 | tf_op jit(solution)/shard_map/all_gather | solution.py:102
  539.0 4.1 collective-permute-start.3
  553.2 2.9 collective-permute-start.5
  557.6 31.9 %copy-start.12 = (bf16[128,2048]{1,0:T(8,128)(2,1)S(1)}, bf16[128,2048]{1,0:T(8,128)(2,1)}, u32[]{:S(2)}) copy-start(bf16[128,2048]{1,0:T(8,128)(2,1)} %copy-done.11) | copy-start | bytes 1572868
  557.6 31.9 %all-to-all-start.16 = ((bf16[4,72,2048]{2,1,0:T(8,128)(2,1)}), bf16[4,72,2048]{2,1,0:T(8,128)(2,1)S(1)}, u32[]{:S(2)}, u32[]{:S(2)}) async-start(bf16[4,72,2048]{2,1,0:T(8,128)(2,1)} %bitcast.50), calls=%async_computation.18 | async-start | bytes 2359296 | tf_op jit(solution)/shard_map/all_to_all | solution.py:83
  561.3 30.1 %copy-start.1 = (bf16[1,128,2048]{2,1,0:T(8,128)(2,1)S(1)}, bf16[1,128,2048]{2,1,0:T(8,128)(2,1)}, u32[]{:S(2)}) copy-start(bf16[1,128,2048]{2,1,0:T(8,128)(2,1)} %param.19) | copy-start | bytes 1572868
  (32 other events, 160.9 us)
Sparse Core Ops, SparseCore 0:
  216.8 27.8 all-gather.6
  246.8 44.8 all-gather.4
  321.3 44.0 reduce-scatter.2
  422.3 26.8 reduce-scatter.4
  465.3 46.1 all-gather.8
  516.7 28.6 all-gather.10
